TPU v7x, 256 devices: a whole 4x4x8 slice. The times are simulated.
256 devices in a mesh: section: 4 (over y), fsdp: 64 (over z, x, core).
Axes of the slice: x: 4, y: 4, z: 8, core: 2. Of those that a mesh axis runs over, the one named last changes fastest.
Arguments:
- residual_input: bfloat16 [2, 4096, 8192], P(None, 'fsdp'), may hold values from -16 to 16
- output_gradient: bfloat16 [2, 4096, 8192], P(None, 'fsdp'), may hold values from -0.0068359375 to 0.0068359375
- value_projection_weight: bfloat16 [4, 8192, 512], P('section', 'fsdp'), may hold values from -0.0625 to 0.0625
- output_weight: bfloat16 [4, 512, 8192], P('section', None, 'fsdp'), may hold values from -0.25 to 0.25
- adapter_down_weight: bfloat16 [4, 8192, 160], P('section'), may hold values from -0.0625 to 0.0625
- adapter_up_weight: bfloat16 [4, 160, 512], P('section'), may hold values from -0.625 to 0.625
- input_norm_scale: float32 [4, 8192], P('section'), may hold values from 0.25 to 1.75
- segment_adapter_index: int32 [2, 128], P(None, 'fsdp'), may hold values from 0 to 3
- adapter_rank_blocks: int32 [4], replicated, may hold values from 1 to 16, 20 in all
Outputs:
- grad_down: float32 [4, 8192, 160], P('section', 'fsdp')
- grad_up: float32 [4, 160, 512], P('section', None, 'fsdp')
Inputs may be any that keep to these rules, and one draw needn't show every extreme that they name: `segment_adapter_index`: adapter of each block of 32 consecutive tokens. `adapter_rank_blocks`: the entries sum to 20.
All inputs are finite; a program needn't handle non-finite values.
Results may differ from a plain program's by a relative error of at most 0.014.
Values may be sent and summed in bfloat16 or wider, within the bound.
No kernel may reach another device: no remote copies, remote signals or barrier semaphores. Data moves between devices by JAX's collectives and lax.ppermute only.
A program may use at most 128 MiB of HBM per device.

v0:
```python
import jax
import jax.numpy as jnp
from jax import lax
from jax.experimental.layout import Layout, with_layout_constraint
from jax.sharding import Mesh, PartitionSpec as P

ADAPTERS = 4
EPSILON = 1e-06
ADAPTER_ALPHA = 32.0
BF = jnp.bfloat16
F32 = jnp.float32
GROUP = ("y", "z", "c")


def contract(left, right, left_dim, right_dim):
    return lax.dot_general(
        left, right, (((left_dim,), (right_dim,)), ((), ())), preferred_element_type=F32
    )


def split_pair(value):
    high = lax.reduce_precision(value, 8, 7)
    return (high.astype(BF), (value - high).astype(BF))


def coefficient_row(adapter, adapter_rank_blocks, columns):
    rank_sizes = 8 * adapter_rank_blocks
    adapters = jnp.arange(ADAPTERS, dtype=jnp.int32)
    ends = jnp.sum(
        jnp.where(adapters[None, :] <= adapters[:, None], rank_sizes[None, :], 0), axis=1
    )
    column = jnp.arange(columns, dtype=jnp.int32)
    owner = jnp.sum((column[:, None] >= ends[None, :]).astype(jnp.int32), axis=1)
    rank = jnp.sum(jnp.where(adapters == adapter, rank_sizes, 0)).astype(F32)
    return jnp.where(owner == adapter, ADAPTER_ALPHA / rank, 0.0)[None, :]


def exchanged(value, axis):
    return lax.all_to_all(value, axis, split_axis=0, concat_axis=0, tiled=True)


def summed(value):
    return value.astype(F32).sum(axis=0)


def gathered_sum(partial):
    return summed(lax.all_gather(partial, "x", axis=0, tiled=False))


def local(
    residual_input,
    output_gradient,
    value_projection_weight,
    output_weight,
    adapter_down_weight,
    adapter_up_weight,
    input_norm_scale,
    segment_adapter_index,
    adapter_rank_blocks,
):
    ny, nz, nx, nc = (lax.axis_size(name) for name in ("y", "z", "x", "c"))
    yi, zi, xi, ci = (lax.axis_index(name) for name in ("y", "z", "x", "c"))
    rows = value_projection_weight.shape[1]
    value_cols = value_projection_weight.shape[2]
    packed = adapter_down_weight.shape[2]
    width = adapter_down_weight.shape[1]
    both = value_cols + packed
    layers = ny
    lanes = nc * rows
    depth = nz * lanes
    joined = jnp.concatenate([value_projection_weight[0], output_weight[0].T], axis=1)
    joined = with_layout_constraint(joined, Layout(major_to_minor=(0, 1)))
    full = lax.all_gather(joined, GROUP, axis=0, tiled=False)
    full = with_layout_constraint(full, Layout(major_to_minor=(0, 1, 2)))
    full = full.reshape(layers, depth, 2 * value_cols)
    value_full = [full[layer, :, :value_cols] for layer in range(layers)]
    out_full = [full[layer, :, value_cols:] for layer in range(layers)]
    all_tokens = residual_input.shape[0] * residual_input.shape[1]
    tokens = all_tokens // ny
    first = yi * tokens
    own = jnp.stack(
        [
            lax.dynamic_slice(array.reshape(all_tokens, width), (first, 0), (tokens, width))
            for array in (residual_input, output_gradient)
        ]
    )
    own = own.reshape(2, tokens, nz, nx, lanes).transpose(3, 0, 1, 2, 4)
    spread = exchanged(own.reshape(nx, 2, tokens, depth), "x")
    state = spread[:, 0].reshape(nx * tokens, depth)
    grad = spread[:, 1].reshape(nx * tokens, depth)
    down_local = lax.dynamic_index_in_dim(
        adapter_down_weight[0].T.reshape(packed, nz, nx, lanes), xi, 2, keepdims=False
    ).reshape(1, packed, depth)
    downs_full = exchanged(jnp.broadcast_to(down_local, (layers, packed, depth)), "y")
    gains_local = lax.dynamic_index_in_dim(
        input_norm_scale.reshape(nz, nx, lanes), xi, 1, keepdims=False
    ).reshape(depth)
    gains = lax.all_gather(gains_local, "y", axis=0, tiled=False)
    ups = lax.all_gather(adapter_up_weight[0], "y", axis=0, tiled=False)
    adapter = lax.dynamic_index_in_dim(segment_adapter_index.reshape(ny), yi, 0, keepdims=False)
    coef_row = coefficient_row(adapter, adapter_rank_blocks, packed)
    coef = lax.all_gather(jnp.broadcast_to(coef_row, (tokens, packed)), "x", axis=0, tiled=True)
    chunk = value_cols // layers
    last = contract(grad, out_full[layers - 1], 1, 0).astype(BF)
    inputs, scaled, projected, inverse, last_sum = ([], [], [], [], [])
    for layer in range(layers):
        widened = state.astype(F32)
        squares = jnp.sum(widened * widened, axis=-1, keepdims=True)
        scaled_input = (widened * gains[layer][None, :]).astype(BF)
        high, low_part = split_pair(squares)
        total = gathered_sum(
            jnp.concatenate(
                [
                    contract(scaled_input, value_full[layer], 1, 0).astype(BF),
                    last[:, layer * chunk : (layer + 1) * chunk],
                    contract(scaled_input, downs_full[layer], 1, 1).astype(BF),
                    high,
                    low_part,
                ],
                axis=1,
            )
        )
        side = value_cols + chunk
        mean = (total[:, side + packed : side + packed + 1] + total[:, side + packed + 1 :]) / width
        inv = lax.rsqrt(mean + EPSILON)
        value_part, low_piece = (total[:, :value_cols], total[:, side : side + packed])
        inputs.append(state)
        scaled.append(scaled_input)
        projected.append((value_part, low_piece))
        inverse.append(inv)
        last_sum.append(total[:, value_cols:side])
        if layer + 1 < layers:
            low = (low_piece * inv * coef).astype(BF)
            value = (value_part * inv + contract(low, ups[layer], 1, 0)).astype(BF)
            state = (widened + contract(value, out_full[layer], 1, 1)).astype(BF)
    blocks = [None] * layers
    extra = -(-packed // rows)
    for layer in reversed(range(layers)):
        if layer + 1 < layers:
            value_sum = gathered_sum(contract(grad, out_full[layer], 1, 0).astype(BF))
        else:
            value_sum = jnp.concatenate(last_sum, axis=1)
        value_grad = value_sum.astype(BF)
        low_grad = (contract(value_grad, ups[layer], 1, 1) * coef).astype(BF)
        inv = inverse[layer]
        value_part, low_piece = projected[layer]
        wide_value, wide_low = (value_grad.astype(F32), low_grad.astype(F32))
        mixed_value, mixed_low = ((wide_value * inv).astype(BF), (wide_low * inv).astype(BF))
        if layer > 0:
            inner = jnp.sum(value_part * wide_value, axis=1, keepdims=True)
            inner = inner + jnp.sum(low_piece * wide_low, axis=1, keepdims=True)
            kappa = inv * inv * inv * inner / width
            back = contract(mixed_value, value_full[layer], 1, 1)
            back = back + contract(mixed_low, downs_full[layer], 1, 0)
            grad = (
                grad.astype(F32) + gains[layer][None, :] * back - kappa * inputs[layer].astype(F32)
            ).astype(BF)
        down = contract(mixed_low, scaled[layer], 0, 0)
        down = down.reshape(packed, nz, nc, rows).transpose(2, 1, 0, 3)
        low = (low_piece * inv * coef).astype(BF)
        chosen = lax.dynamic_index_in_dim(
            value_grad.reshape(nx * tokens, nz, nx, -1), xi, 2, keepdims=False
        )
        each = chosen.shape[2] // nc
        up = contract(chosen.reshape(nx * tokens, -1), low, 0, 0)
        up = up.reshape(nz, nc, each, packed).transpose(1, 0, 2, 3)
        up = jnp.pad(up, ((0, 0), (0, 0), (0, 0), (0, extra * rows - packed)))
        block = jnp.concatenate(
            [down] + [up[..., k * rows : (k + 1) * rows] for k in range(extra)], axis=2
        ).astype(BF)
        blocks[layer] = summed(exchanged(block, "c")).astype(BF)
    total = summed(exchanged(jnp.stack(blocks), "y")).astype(BF)
    total = summed(exchanged(total, "z"))
    up = jnp.concatenate(
        [total[packed + k * each : packed + (k + 1) * each] for k in range(extra)], axis=1
    )[:, :packed]
    return (total[:packed].T[None], up.T[None])


def solution(mesh):
    shape = mesh.devices.shape
    cores, across = (2, 4)
    split = Mesh(
        mesh.devices.reshape(shape[0], shape[1] // (across * cores), across, cores),
        ("y", "z", "x", "c"),
    )
    fsdp = ("z", "x", "c")
    placed = (
        P(None, fsdp, None),
        P(None, fsdp, None),
        P("y", fsdp, None),
        P("y", None, fsdp),
        P("y", None, None),
        P("y", None, None),
        P("y", None),
        P(None, fsdp),
        P(),
    )
    return jax.shard_map(
        local,
        mesh=split,
        in_specs=placed,
        out_specs=(P("y", fsdp, None), P("y", None, fsdp)),
        check_vma=False,
    )
```

profile of v0, /device:TPU:2, one launch (start us, length us, event | category | flops | bytes accessed | tf_op | source)
XLA Modules:
  0.0 391.7 jit_solution(12321162908527013947)
XLA Ops:
  14.2 5.7 %all-to-all-start = ((bf16[4,2,32,2048]{3,2,1,0:T(8,128)(2,1)}), bf16[4,2,32,2048]{3,2,1,0:T(8,128)(2,1)S(1)}, u32[]{:S(2)}, u32[]{:S(2)}) async-start(bf16[4,2,32,2048]{3,2,1,0:T(8,128)(2,1)} %reshape.261), calls=%async_computation | async-start | bytes 2097152 | tf_op jit(solution)/shard_map/all_to_all | solution.py:39
  23.8 5.5 %reshape.264 = bf16[160,8,4,256]{3,2,1,0:T(4,128)(2,1)} reshape(bf16[160,8192]{1,0:T(8,128)(2,1)} %bitcast.315) | data formatting | bytes 5242880 | tf_op jit(solution)/shard_map/reshape | solution.py:92
  29.3 5.6 %dynamic-slice_reduce_fusion = bf16[160,8,256]{2,1,0:T(8,128)(2,1)S(1)} fusion(bf16[160,8,4,256]{3,2,1,0:T(4,128)(2,1)} %reshape.264, s32[]{:T(128)S(6)} %select_n.36), kind=kLoop, calls=%fused_computation.52 | loop fusion | bytes 1310724 | tf_op jit(solution)/shard_map/jit(dynamic_index_in_dim)/dynamic_slice | solution.py:91
  36.0 13.0 %all_gather.63 = bf16[4,160,512]{2,1,0:T(8,128)(2,1)S(1)} all-gather(bf16[1,160,512]{2,1,0:T(8,128)(2,1)S(1)} %copy-done.30), channel_id=1, replica_groups=mesh['y'=4,'z'=8,'x'=4,'c'=2] {'y'}, dimensions={0}, use_global_device_ids=true | all-gather | bytes 819200 | tf_op jit(solution)/shard_map/all_gather | solution.py:99
  50.9 4.6 %all-to-all-start.1 = ((bf16[4,160,2048]{2,1,0:T(8,128)(2,1)}), bf16[4,160,2048]{2,1,0:T(8,128)(2,1)}, u32[]{:S(2)}, u32[]{:S(2)}) async-start(bf16[4,160,2048]{2,1,0:T(8,128)(2,1)} %broadcast_in_dim.35), calls=%async_computation.1 | async-start | bytes 5242880 | tf_op jit(solution)/shard_map/all_to_all | solution.py:39
  55.5 12.0 %all_gather.62 = f32[128,160]{1,0:T(8,128)S(1)} all-gather(f32[32,160]{1,0:T(8,128)S(1)} %broadcast_in_dim.65), channel_id=1, replica_groups=mesh['y'=4,'z'=8,'x'=4,'c'=2] {'x'}, dimensions={0}, use_global_device_ids=true | all-gather | bytes 102400 | tf_op jit(solution)/shard_map/all_gather | solution.py:102
  67.6 44.8 %all-gather.8 = f32[4,1,2048]{2,1,0:T(1,128)S(1)} all-gather(f32[1,1,2048]{2,1,0:T(1,128)S(1)} %bitcast.353), channel_id=1, replica_groups=mesh['y'=4,'z'=8,'x'=4,'c'=2] {'y'}, dimensions={0}, use_global_device_ids=true | all-gather | bytes 40960 | tf_op jit(solution)/shard_map/all_gather | solution.py:98
  117.5 17.1 %all-gather.11.cloned.1.call-done = bf16[8192,1024]{1,0:T(8,128)(2,1)} async-done(((bf16[128,1024]{1,0:T(8,128)(2,1)}), bf16[8192,1024]{1,0:T(8,128)(2,1)}) %all-gather.11.cloned.1.call-update) | async-done | bytes 16777232 | tf_op jit(solution)/shard_map/all_gather | solution.py:73
  139.6 14.7 %all-gather.1 = bf16[512,802]{1,0:T(8,128)(2,1)S(1)} all-gather(bf16[128,802]{1,0:T(8,128)(2,1)S(1)} %concatenate.52), channel_id=3, replica_groups=mesh['y'=4,'z'=8,'x'=4,'c'=2] {'x'}, dimensions={0}, use_global_device_ids=true | all-gather | bytes 1026560 | tf_op jit(solution)/shard_map/all_gather | solution.py:47
  154.8 3.3 multiply_reduce_fusion.2
  162.4 13.8 %all-gather.2 = bf16[512,802]{1,0:T(8,128)(2,1)S(1)} all-gather(bf16[128,802]{1,0:T(8,128)(2,1)S(1)} %concatenate.53), channel_id=4, replica_groups=mesh['y'=4,'z'=8,'x'=4,'c'=2] {'x'}, dimensions={0}, use_global_device_ids=true | all-gather | bytes 1026560 | tf_op jit(solution)/shard_map/all_gather | solution.py:47
  177.2 3.4 multiply_reduce_fusion.1
  184.8 14.2 %all-gather.3 = bf16[512,802]{1,0:T(8,128)(2,1)S(1)} all-gather(bf16[128,802]{1,0:T(8,128)(2,1)S(1)} %concatenate.54), channel_id=5, replica_groups=mesh['y'=4,'z'=8,'x'=4,'c'=2] {'x'}, dimensions={0}, use_global_device_ids=true | all-gather | bytes 1026560 | tf_op jit(solution)/shard_map/all_gather | solution.py:47
  205.6 3.5 multiply_reduce_fusion
  210.6 2.9 fusion.33
  216.7 13.6 %all-gather.4 = bf16[512,802]{1,0:T(8,128)(2,1)S(1)} all-gather(bf16[128,802]{1,0:T(8,128)(2,1)S(1)} %concatenate.55), channel_id=6, replica_groups=mesh['y'=4,'z'=8,'x'=4,'c'=2] {'x'}, dimensions={0}, use_global_device_ids=true | all-gather | bytes 1026560 | tf_op jit(solution)/shard_map/all_gather | solution.py:47
  238.8 2.5 fusion.27
  246.2 12.8 %all-gather.5 = bf16[512,512]{1,0:T(8,128)(2,1)S(1)} all-gather(bf16[128,512]{1,0:T(8,128)(2,1)S(1)} %fusion.34), channel_id=7, replica_groups=mesh['y'=4,'z'=8,'x'=4,'c'=2] {'x'}, dimensions={0}, use_global_device_ids=true | all-gather | bytes 655360 | tf_op jit(solution)/shard_map/all_gather | solution.py:47
  262.8 2.5 fusion.24
  268.1 2.2 fusion.36
  270.3 12.8 %all-gather.6 = bf16[512,512]{1,0:T(8,128)(2,1)S(1)} all-gather(bf16[128,512]{1,0:T(8,128)(2,1)S(1)} %fusion.36), channel_id=8, replica_groups=mesh['y'=4,'z'=8,'x'=4,'c'=2] {'x'}, dimensions={0}, use_global_device_ids=true | all-gather | bytes 655360 | tf_op jit(solution)/shard_map/all_gather | solution.py:47
  286.0 2.4 fusion.21
  288.7 2.3 reshape.274
  291.2 4.3 %all_to_all.40 = bf16[2,8,176,128]{3,1,2,0:T(8,128)(2,1)S(1)} all-to-all(bf16[2,8,176,128]{3,1,2,0:T(8,128)(2,1)S(1)} %pad_maximum_fusion.4), channel_id=1, replica_groups=mesh['y'=4,'z'=8,'x'=4,'c'=2] {'c'}, dimensions={0} | all-to-all | bytes 1441792 | tf_op jit(solution)/shard_map/all_to_all | solution.py:39
  298.3 2.3 reshape.271
  301.8 4.5 %all_to_all.41 = bf16[2,8,176,128]{3,1,2,0:T(8,128)(2,1)S(1)} all-to-all(bf16[2,8,176,128]{3,1,2,0:T(8,128)(2,1)S(1)} %pad_maximum_fusion.3), channel_id=1, replica_groups=mesh['y'=4,'z'=8,'x'=4,'c'=2] {'c'}, dimensions={0} | all-to-all | bytes 1441792 | tf_op jit(solution)/shard_map/all_to_all | solution.py:39
  314.1 4.3 %all_to_all.42 = bf16[2,8,176,128]{3,1,2,0:T(8,128)(2,1)S(1)} all-to-all(bf16[2,8,176,128]{3,1,2,0:T(8,128)(2,1)S(1)} %pad_maximum_fusion.2), channel_id=1, replica_groups=mesh['y'=4,'z'=8,'x'=4,'c'=2] {'c'}, dimensions={0} | all-to-all | bytes 1441792 | tf_op jit(solution)/shard_map/all_to_all | solution.py:39
  321.9 2.7 fusion.38
  324.6 12.8 %all-gather.7 = bf16[512,512]{1,0:T(8,128)(2,1)S(1)} all-gather(bf16[128,512]{1,0:T(8,128)(2,1)S(1)} %fusion.38), channel_id=9, replica_groups=mesh['y'=4,'z'=8,'x'=4,'c'=2] {'x'}, dimensions={0}, use_global_device_ids=true | all-gather | bytes 655360 | tf_op jit(solution)/shard_map/all_gather | solution.py:47
  338.6 4.4 %all_to_all.43 = bf16[2,8,176,128]{3,2,1,0:T(8,128)(2,1)S(1)} all-to-all(bf16[2,8,176,128]{3,2,1,0:T(8,128)(2,1)S(1)} %copy.412), channel_id=1, replica_groups=mesh['y'=4,'z'=8,'x'=4,'c'=2] {'c'}, dimensions={0} | all-to-all | bytes 1441792 | tf_op jit(solution)/shard_map/all_to_all | solution.py:39
  343.4 22.3 %all_to_all.44 = bf16[4,8,176,128]{3,2,1,0:T(8,128)(2,1)S(1)} all-to-all(bf16[4,8,176,128]{3,2,1,0:T(8,128)(2,1)S(1)} %pad_maximum_fusion), channel_id=1, replica_groups=mesh['y'=4,'z'=8,'x'=4,'c'=2] {'y'}, dimensions={0} | all-to-all | bytes 2883584 | tf_op jit(solution)/shard_map/all_to_all | solution.py:39
  366.0 17.5 %all_to_all.45 = bf16[8,176,128]{2,1,0:T(8,128)(2,1)S(1)} all-to-all(bf16[8,176,128]{2,1,0:T(8,128)(2,1)S(1)} %reduce_sum.294), channel_id=1, replica_groups=mesh['y'=4,'z'=8,'x'=4,'c'=2] {'z'}, dimensions={0} | all-to-all | bytes 720896 | tf_op jit(solution)/shard_map/all_to_all | solution.py:39
  (271 shorter events, 85.4 us)
Async XLA Ops:
  7.2 127.4 %all-gather.11.cloned.1.call-start = ((), (), s32[]{:S(2)}) async-start(), calls=%async_computation.8 | async-start | bytes 17039360 | tf_op jit(solution)/shard_map/all_gather | solution.py:73
  12.8 7.1 %copy-start.56 = (s32[2,2]{1,0:T(2,128)S(1)}, s32[2,2]{1,0:T(2,128)}, u32[]{:S(2)}) copy-start(s32[2,2]{1,0:T(2,128)} %param.16) | copy-start | bytes 52
  12.8 7.7 %copy-start.55 = (s32[4]{0:T(128)S(1)}, s32[4]{0:T(128)}, u32[]{:S(2)}) copy-start(s32[4]{0:T(128)} %param.17) | copy-start | bytes 52
  12.9 10.2 %copy-start.40 = (f32[1,8192]{1,0:T(1,128)S(1)}, f32[1,8192]{1,0:T(1,128)}, u32[]{:S(2)}) copy-start(f32[1,8192]{1,0:T(1,128)} %param.15) | copy-start | bytes 98308
  14.2 34.9 %all-to-all-start = ((bf16[4,2,32,2048]{3,2,1,0:T(8,128)(2,1)}), bf16[4,2,32,2048]{3,2,1,0:T(8,128)(2,1)S(1)}, u32[]{:S(2)}, u32[]{:S(2)}) async-start(bf16[4,2,32,2048]{3,2,1,0:T(8,128)(2,1)} %reshape.261), calls=%async_computation | async-start | bytes 2097152 | tf_op jit(solution)/shard_map/all_to_all | solution.py:39
  29.3 6.7 %copy-start.30 = (bf16[1,160,512]{2,1,0:T(8,128)(2,1)S(1)}, bf16[1,160,512]{2,1,0:T(8,128)(2,1)}, u32[]{:S(2)}) copy-start(bf16[1,160,512]{2,1,0:T(8,128)(2,1)} %param.14) | copy-start | bytes 491524
  49.0 128.2 %copy-start = (bf16[4,160,512]{2,1,0:T(8,128)(2,1)}, bf16[4,160,512]{2,1,0:T(8,128)(2,1)S(1)}, u32[]{:S(2)}) copy-start(bf16[4,160,512]{2,1,0:T(8,128)(2,1)S(1)} %all_gather.63) | copy-start | bytes 1966084
  50.9 64.7 %all-to-all-start.1 = ((bf16[4,160,2048]{2,1,0:T(8,128)(2,1)}), bf16[4,160,2048]{2,1,0:T(8,128)(2,1)}, u32[]{:S(2)}, u32[]{:S(2)}) async-start(bf16[4,160,2048]{2,1,0:T(8,128)(2,1)} %broadcast_in_dim.35), calls=%async_computation.1 | async-start | bytes 5242880 | tf_op jit(solution)/shard_map/all_to_all | solution.py:39
  113.0 41.9 %copy-start.35 = (f32[1,1,2048]{2,1,0:T(1,128)}, f32[1,1,2048]{2,1,0:T(1,128)S(1)}, u32[]{:S(2)}) copy-start(f32[1,1,2048]{2,1,0:T(1,128)S(1)} %get-tuple-element.35) | copy-start | bytes 24580
  113.0 64.2 %copy-start.36 = (f32[1,1,2048]{2,1,0:T(1,128)}, f32[1,1,2048]{2,1,0:T(1,128)S(1)}, u32[]{:S(2)}) copy-start(f32[1,1,2048]{2,1,0:T(1,128)S(1)} %get-tuple-element.37) | copy-start | bytes 24580
  115.6 21.2 %copy-start.5 = (bf16[4,1,32,2048]{3,2,1,0:T(8,128)(2,1)}, bf16[4,1,32,2048]{3,2,1,0:T(8,128)(2,1)S(1)}, u32[]{:S(2)}) copy-start(bf16[4,1,32,2048]{3,2,1,0:T(8,128)(2,1)S(1)} %get-tuple-element.10) | copy-start | bytes 1572868
  184.7 20.9 %copy-start.38 = (f32[1,1,2048]{2,1,0:T(1,128)S(1)}, f32[1,1,2048]{2,1,0:T(1,128)}, u32[]{:S(2)}) copy-start(f32[1,1,2048]{2,1,0:T(1,128)} %get-tuple-element.34) | copy-start | bytes 24580
  244.0 15.1 %copy-start.8 = (bf16[128,2048]{1,0:T(8,128)(2,1)}, bf16[128,2048]{1,0:T(8,128)(2,1)S(1)}, u32[]{:S(2)}) copy-start(bf16[128,2048]{1,0:T(8,128)(2,1)S(1)} %fusion.15) | copy-start | bytes 1572868
  244.0 16.2 %copy-start.1 = (bf16[4,160,512]{2,1,0:T(8,128)(2,1)S(1)}, bf16[4,160,512]{2,1,0:T(8,128)(2,1)}, u32[]{:S(2)}) copy-start(bf16[4,160,512]{2,1,0:T(8,128)(2,1)} %copy-done) | copy-start | bytes 1966084
  244.0 18.8 %copy-start.44 = (f32[128]{0:T(128)S(1)}, f32[128]{0:T(128)}, u32[]{:S(2)}) copy-start(f32[128]{0:T(128)} %copy-done.43) | copy-start | bytes 1540
  260.2 5.1 %copy-start.13 = (bf16[128,2048]{1,0:T(8,128)(2,1)S(1)}, bf16[128,2048]{1,0:T(8,128)(2,1)}, u32[]{:S(2)}) copy-start(bf16[128,2048]{1,0:T(8,128)(2,1)} %get-tuple-element.5) | copy-start | bytes 1572868
  268.0 15.1 %copy-start.7 = (bf16[128,2048]{1,0:T(8,128)(2,1)}, bf16[128,2048]{1,0:T(8,128)(2,1)S(1)}, u32[]{:S(2)}) copy-start(bf16[128,2048]{1,0:T(8,128)(2,1)S(1)} %fusion.16) | copy-start | bytes 1572868
  268.0 15.1 %copy-start.3 = (f32[128,802]{1,0:T(8,128)S(1)}, f32[128,802]{1,0:T(8,128)}, u32[]{:S(2)}) copy-start(f32[128,802]{1,0:T(8,128)} %copy-done.2) | copy-start | bytes 1231876
  268.0 15.8 %copy-start.20 = (f32[128,160]{0,1:T(8,128)S(1)}, f32[128,160]{0,1:T(8,128)}, u32[]{:S(2)}) copy-start(f32[128,160]{0,1:T(8,128)} %copy-done.19) | copy-start | bytes 245764
  268.1 18.0 %copy-start.42 = (f32[128]{0:T(128)S(1)}, f32[128]{0:T(128)}, u32[]{:S(2)}) copy-start(f32[128]{0:T(128)} %copy-done.41) | copy-start | bytes 1540
  283.9 4.5 %copy-start.29 = (f32[128,160]{0,1:T(8,128)S(1)}, f32[128,160]{0,1:T(8,128)}, u32[]{:S(2)}) copy-start(f32[128,160]{0,1:T(8,128)} %copy.460) | copy-start | bytes 245764
  283.9 4.5 %copy-start.31 = (bf16[128,128]{0,1:T(8,128)(2,1)S(1)}, bf16[128,128]{0,1:T(8,128)(2,1)}, u32[]{:S(2)}) copy-start(bf16[128,128]{0,1:T(8,128)(2,1)} %copy.426) | copy-start | bytes 98308
  283.9 4.5 %copy-start.32 = (bf16[128,128]{0,1:T(8,128)(2,1)S(1)}, bf16[128,128]{0,1:T(8,128)(2,1)}, u32[]{:S(2)}) copy-start(bf16[128,128]{0,1:T(8,128)(2,1)} %copy.427) | copy-start | bytes 98308
  283.9 4.5 %copy-start.33 = (bf16[128,128]{0,1:T(8,128)(2,1)S(1)}, bf16[128,128]{0,1:T(8,128)(2,1)}, u32[]{:S(2)}) copy-start(bf16[128,128]{0,1:T(8,128)(2,1)} %copy.428) | copy-start | bytes 98308
  283.9 4.5 %copy-start.34 = (bf16[128,128]{0,1:T(8,128)(2,1)S(1)}, bf16[128,128]{0,1:T(8,128)(2,1)}, u32[]{:S(2)}) copy-start(bf16[128,128]{0,1:T(8,128)(2,1)} %copy.429) | copy-start | bytes 98308
  283.9 4.5 %copy-start.46 = (f32[128]{0:T(128)S(1)}, f32[128]{0:T(128)}, u32[]{:S(2)}) copy-start(f32[128]{0:T(128)} %copy-done.45) | copy-start | bytes 1540
  321.9 15.7 %copy-start.10 = (bf16[2048,128]{1,0:T(8,128)(2,1)S(1)}, bf16[2048,128]{1,0:T(8,128)(2,1)}, u32[]{:S(2)}) copy-start(bf16[2048,128]{1,0:T(8,128)(2,1)} %copy.442) | copy-start | bytes 1572868
  321.9 15.7 %copy-start.48 = (f32[128]{0:T(128)S(1)}, f32[128]{0:T(128)}, u32[]{:S(2)}) copy-start(f32[128]{0:T(128)} %copy-done.47) | copy-start | bytes 1540
  324.6 13.6 %copy-start.24 = (bf16[128,160]{0,1:T(8,128)(2,1)S(1)}, bf16[128,160]{0,1:T(8,128)(2,1)}, u32[]{:S(2)}) copy-start(bf16[128,160]{0,1:T(8,128)(2,1)} %copy-done.23) | copy-start | bytes 122884
  338.5 4.8 %copy-start.16 = (bf16[8,176,128]{2,1,0:T(8,128)(2,1)S(1)}, bf16[8,176,128]{2,1,0:T(8,128)(2,1)}, u32[]{:S(2)}) copy-start(bf16[8,176,128]{2,1,0:T(8,128)(2,1)} %copy.471) | copy-start | bytes 1081348
  338.5 4.8 %copy-start.17 = (bf16[8,176,128]{2,1,0:T(8,128)(2,1)S(1)}, bf16[8,176,128]{2,1,0:T(8,128)(2,1)}, u32[]{:S(2)}) copy-start(bf16[8,176,128]{2,1,0:T(8,128)(2,1)} %copy.472) | copy-start | bytes 1081348
  338.5 4.8 %copy-start.18 = (bf16[8,176,128]{2,1,0:T(8,128)(2,1)S(1)}, bf16[8,176,128]{2,1,0:T(8,128)(2,1)}, u32[]{:S(2)}) copy-start(bf16[8,176,128]{2,1,0:T(8,128)(2,1)} %copy.473) | copy-start | bytes 1081348
  (28 other events, 82.5 us)
Sparse Core Ops, SparseCore 0:
  10.7 123.7 all-gather.10
where the time goes:
time: 394 us; the launch traced here: 392 us
  blocking collectives  222 us (56%)
  matrix products  56.4 us (14%)
  local copies, waits for them, and re-layouts  53.8 us (14%)
  waiting for transfers between devices  17.1 us (4%)
  other arithmetic  16.3 us (4%)
  between operations  16 us (4%)
  starting transfers between devices  10.3 us (3%)
    all_gather x7, blocking collectives, gathered_sum(): return summed(lax.all_gather(partial, 'x', axis=0, tiled=False))  94.5 us
    all_to_all x6, blocking collectives, exchanged(): return lax.all_to_all(value, axis, split_axis=0, concat_axis=0, tiled=True)  57.5 us
    dot_general x31, matrix products, contract(): lax.dot_general(left, right, (((left_dim,), (right_dim,)), ((), ())), pre...  56.4 us
    all_gather x1, blocking collectives, local(): gains = lax.all_gather(gains_local, 'y', axis=0, tiled=False)  44.8 us
    all_gather x1, waiting for transfers between devices, local(): full = lax.all_gather(joined, GROUP, axis=0, tiled=False)  17.1 us
    all_gather x1, blocking collectives, local(): ups = lax.all_gather(adapter_up_weight[0], 'y', axis=0, tiled=False)  13 us
    all_gather x1, blocking collectives, local(): lax.all_gather(jnp.broadcast_to(coef_row, (tokens, packed)), 'x', axis=0,...  12 us
    all_to_all x2, starting transfers between devices, exchanged(): return lax.all_to_all(value, axis, split_axis=0, concat_axis=0, tiled=True)  10.3 us
  transfers between devices with their start and end apart: 3, of which 1 were waited for; matrix products, arithmetic and copies ran while one was open for 7% of the time, Pallas kernels for 0%

commit v1 on v0

--- a/solution.py
+++ b/solution.py
@@ -99,7 +99,15 @@
     ups = lax.all_gather(adapter_up_weight[0], "y", axis=0, tiled=False)
     adapter = lax.dynamic_index_in_dim(segment_adapter_index.reshape(ny), yi, 0, keepdims=False)
     coef_row = coefficient_row(adapter, adapter_rank_blocks, packed)
-    coef = lax.all_gather(jnp.broadcast_to(coef_row, (tokens, packed)), "x", axis=0, tiled=True)
+    coef = jnp.concatenate(
+        lax.all_to_all(
+            jnp.stack([jnp.broadcast_to(coef_row, (tokens, packed))] * lax.axis_size("x")),
+            "x",
+            0,
+            0,
+        ),
+        axis=0,
+    )
     chunk = value_cols // layers
     last = contract(grad, out_full[layers - 1], 1, 0).astype(BF)
     inputs, scaled, projected, inverse, last_sum = ([], [], [], [], [])

time: 394 us -> 399 us (1.013)
  waiting for transfers between devices: 17.1 us -> 9.47 us
  blocking collectives: 222 us -> 227 us
  starting transfers between devices: 10.3 us -> 15.1 us
    all_gather x1, blocking collectives: 44.8 us -> 61.8 us  [local(): gains = lax.all_gather(gains_local, 'y', axis=0, tiled=False)]
    all_gather x1 -> x0, blocking collectives: 12 us -> none  [local(): lax.all_gather(jnp.broadcast_to(coef_row, (tokens, packed)), 'x', axis=0,...]
    all_gather x1, waiting for transfers between devices: 17.1 us -> 9.17 us  [local(): full = lax.all_gather(joined, GROUP, axis=0, tiled=False)]
    all_to_all x0 -> x1, starting transfers between devices: none -> 5.53 us  [local(): lax.all_to_all(jnp.stack([jnp.broadcast_to(coef_row, (tokens, packed))] *...]
  transfers between devices with their start and end apart: 3 -> 4, of which waited for: 1 -> 2; matrix products, arithmetic and copies ran while one was open for 7% -> 7% of each run, Pallas kernels for 0% -> 0%
where the time goes in v1:
time: 399 us; the launch traced here: 396 us
  blocking collectives  227 us (57%)
  matrix products  56.4 us (14%)
  local copies, waits for them, and re-layouts  55.1 us (14%)
  other arithmetic  17 us (4%)
  between operations  15.9 us (4%)
  starting transfers between devices  15.1 us (4%)
  waiting for transfers between devices  9.47 us (2%)
    all_gather x7, blocking collectives, gathered_sum(): return summed(lax.all_gather(partial, 'x', axis=0, tiled=False))  95.4 us
    all_gather x1, blocking collectives, local(): gains = lax.all_gather(gains_local, 'y', axis=0, tiled=False)  61.8 us
    dot_general x31, matrix products, contract(): lax.dot_general(left, right, (((left_dim,), (right_dim,)), ((), ())), pre...  56.4 us
    all_to_all x6, blocking collectives, exchanged(): return lax.all_to_all(value, axis, split_axis=0, concat_axis=0, tiled=True)  56.2 us
    all_gather x1, blocking collectives, local(): ups = lax.all_gather(adapter_up_weight[0], 'y', axis=0, tiled=False)  13.8 us
    all_to_all x2, starting transfers between devices, exchanged(): return lax.all_to_all(value, axis, split_axis=0, concat_axis=0, tiled=True)  9.5 us
    all_gather x1, waiting for transfers between devices, local(): full = lax.all_gather(joined, GROUP, axis=0, tiled=False)  9.17 us
  transfers between devices with their start and end apart: 4, of which 2 were waited for; matrix products, arithmetic and copies ran while one was open for 7% of the time, Pallas kernels for 0%

profile of v1, /device:TPU:2, one launch (start us, length us, event | category | flops | bytes accessed | tf_op | source)
XLA Modules:
  0.0 396.2 jit_solution(16052977591796032692)
XLA Ops:
  15.4 5.5 %all-to-all-start.2 = ((f32[4,32,160]{2,1,0:T(8,128)}), f32[4,32,160]{2,1,0:T(8,128)S(1)}, u32[]{:S(2)}, u32[]{:S(2)}) async-start(f32[4,32,160]{2,1,0:T(8,128)} %stack.30), calls=%async_computation.2 | async-start | bytes 262144 | tf_op jit(solution)/shard_map/all_to_all | solution.py:103
  25.5 4.9 %all-to-all-start = ((bf16[4,2,32,2048]{3,2,1,0:T(8,128)(2,1)}), bf16[4,2,32,2048]{3,2,1,0:T(8,128)(2,1)S(1)}, u32[]{:S(2)}, u32[]{:S(2)}) async-start(bf16[4,2,32,2048]{3,2,1,0:T(8,128)(2,1)} %reshape.261), calls=%async_computation | async-start | bytes 2097152 | tf_op jit(solution)/shard_map/all_to_all | solution.py:39
  31.7 5.5 %reshape.264 = bf16[160,8,4,256]{3,2,1,0:T(4,128)(2,1)} reshape(bf16[160,8192]{1,0:T(8,128)(2,1)} %bitcast.316) | data formatting | bytes 5242880 | tf_op jit(solution)/shard_map/reshape | solution.py:92
  37.2 5.6 %dynamic-slice_reduce_fusion = bf16[160,8,256]{2,1,0:T(8,128)(2,1)S(1)} fusion(bf16[160,8,4,256]{3,2,1,0:T(4,128)(2,1)} %reshape.264, s32[]{:T(128)S(6)} %select_n.32), kind=kLoop, calls=%fused_computation.52 | loop fusion | bytes 1310724 | tf_op jit(solution)/shard_map/jit(dynamic_index_in_dim)/dynamic_slice | solution.py:91
  43.0 13.8 %all_gather.59 = bf16[4,160,512]{2,1,0:T(8,128)(2,1)S(1)} all-gather(bf16[1,160,512]{2,1,0:T(8,128)(2,1)S(1)} %copy-done.30), channel_id=1, replica_groups=mesh['y'=4,'z'=8,'x'=4,'c'=2] {'y'}, dimensions={0}, use_global_device_ids=true | all-gather | bytes 819200 | tf_op jit(solution)/shard_map/all_gather | solution.py:99
  58.6 4.6 %all-to-all-start.1 = ((bf16[4,160,2048]{2,1,0:T(8,128)(2,1)}), bf16[4,160,2048]{2,1,0:T(8,128)(2,1)}, u32[]{:S(2)}, u32[]{:S(2)}) async-start(bf16[4,160,2048]{2,1,0:T(8,128)(2,1)} %broadcast_in_dim.33), calls=%async_computation.1 | async-start | bytes 5242880 | tf_op jit(solution)/shard_map/all_to_all | solution.py:39
  63.2 61.8 %all-gather.8 = f32[4,1,2048]{2,1,0:T(1,128)S(1)} all-gather(f32[1,1,2048]{2,1,0:T(1,128)S(1)} %bitcast.355), channel_id=1, replica_groups=mesh['y'=4,'z'=8,'x'=4,'c'=2] {'y'}, dimensions={0}, use_global_device_ids=true | all-gather | bytes 40960 | tf_op jit(solution)/shard_map/all_gather | solution.py:98
  130.2 9.2 %all-gather.11.cloned.1.call-done = bf16[8192,1024]{1,0:T(8,128)(2,1)} async-done(((bf16[128,1024]{1,0:T(8,128)(2,1)}), bf16[8192,1024]{1,0:T(8,128)(2,1)}) %all-gather.11.cloned.1.call-update) | async-done | bytes 16777232 | tf_op jit(solution)/shard_map/all_gather | solution.py:73
  144.4 15.0 %all-gather.1 = bf16[512,802]{1,0:T(8,128)(2,1)S(1)} all-gather(bf16[128,802]{1,0:T(8,128)(2,1)S(1)} %concatenate.52), channel_id=3, replica_groups=mesh['y'=4,'z'=8,'x'=4,'c'=2] {'x'}, dimensions={0}, use_global_device_ids=true | all-gather | bytes 1026560 | tf_op jit(solution)/shard_map/all_gather | solution.py:47
  159.9 3.3 multiply_reduce_fusion.2
  167.5 13.8 %all-gather.2 = bf16[512,802]{1,0:T(8,128)(2,1)S(1)} all-gather(bf16[128,802]{1,0:T(8,128)(2,1)S(1)} %concatenate.53), channel_id=4, replica_groups=mesh['y'=4,'z'=8,'x'=4,'c'=2] {'x'}, dimensions={0}, use_global_device_ids=true | all-gather | bytes 1026560 | tf_op jit(solution)/shard_map/all_gather | solution.py:47
  182.3 3.4 multiply_reduce_fusion.1
  189.9 14.4 %all-gather.3 = bf16[512,802]{1,0:T(8,128)(2,1)S(1)} all-gather(bf16[128,802]{1,0:T(8,128)(2,1)S(1)} %concatenate.54), channel_id=5, replica_groups=mesh['y'=4,'z'=8,'x'=4,'c'=2] {'x'}, dimensions={0}, use_global_device_ids=true | all-gather | bytes 1026560 | tf_op jit(solution)/shard_map/all_gather | solution.py:47
  210.9 3.5 multiply_reduce_fusion
  215.9 2.9 fusion.33
  222.0 13.6 %all-gather.4 = bf16[512,802]{1,0:T(8,128)(2,1)S(1)} all-gather(bf16[128,802]{1,0:T(8,128)(2,1)S(1)} %concatenate.55), channel_id=6, replica_groups=mesh['y'=4,'z'=8,'x'=4,'c'=2] {'x'}, dimensions={0}, use_global_device_ids=true | all-gather | bytes 1026560 | tf_op jit(solution)/shard_map/all_gather | solution.py:47
  244.1 2.5 fusion.27
  251.5 12.8 %all-gather.5 = bf16[512,512]{1,0:T(8,128)(2,1)S(1)} all-gather(bf16[128,512]{1,0:T(8,128)(2,1)S(1)} %fusion.34), channel_id=7, replica_groups=mesh['y'=4,'z'=8,'x'=4,'c'=2] {'x'}, dimensions={0}, use_global_device_ids=true | all-gather | bytes 655360 | tf_op jit(solution)/shard_map/all_gather | solution.py:47
  268.1 2.5 fusion.24
  273.4 2.2 fusion.36
  275.6 12.8 %all-gather.6 = bf16[512,512]{1,0:T(8,128)(2,1)S(1)} all-gather(bf16[128,512]{1,0:T(8,128)(2,1)S(1)} %fusion.36), channel_id=8, replica_groups=mesh['y'=4,'z'=8,'x'=4,'c'=2] {'x'}, dimensions={0}, use_global_device_ids=true | all-gather | bytes 655360 | tf_op jit(solution)/shard_map/all_gather | solution.py:47
  291.3 2.4 fusion.21
  294.0 2.3 reshape.275
  296.5 4.3 %all_to_all.45 = bf16[2,8,176,128]{3,1,2,0:T(8,128)(2,1)S(1)} all-to-all(bf16[2,8,176,128]{3,1,2,0:T(8,128)(2,1)S(1)} %pad_maximum_fusion.4), channel_id=1, replica_groups=mesh['y'=4,'z'=8,'x'=4,'c'=2] {'c'}, dimensions={0} | all-to-all | bytes 1441792 | tf_op jit(solution)/shard_map/all_to_all | solution.py:39
  303.6 2.3 reshape.272
  307.1 4.5 %all_to_all.46 = bf16[2,8,176,128]{3,1,2,0:T(8,128)(2,1)S(1)} all-to-all(bf16[2,8,176,128]{3,1,2,0:T(8,128)(2,1)S(1)} %pad_maximum_fusion.3), channel_id=1, replica_groups=mesh['y'=4,'z'=8,'x'=4,'c'=2] {'c'}, dimensions={0} | all-to-all | bytes 1441792 | tf_op jit(solution)/shard_map/all_to_all | solution.py:39
  319.4 4.3 %all_to_all.47 = bf16[2,8,176,128]{3,1,2,0:T(8,128)(2,1)S(1)} all-to-all(bf16[2,8,176,128]{3,1,2,0:T(8,128)(2,1)S(1)} %pad_maximum_fusion.2), channel_id=1, replica_groups=mesh['y'=4,'z'=8,'x'=4,'c'=2] {'c'}, dimensions={0} | all-to-all | bytes 1441792 | tf_op jit(solution)/shard_map/all_to_all | solution.py:39
  327.2 2.7 fusion.38
  329.9 13.2 %all-gather.7 = bf16[512,512]{1,0:T(8,128)(2,1)S(1)} all-gather(bf16[128,512]{1,0:T(8,128)(2,1)S(1)} %fusion.38), channel_id=9, replica_groups=mesh['y'=4,'z'=8,'x'=4,'c'=2] {'x'}, dimensions={0}, use_global_device_ids=true | all-gather | bytes 655360 | tf_op jit(solution)/shard_map/all_gather | solution.py:47
  344.3 4.4 %all_to_all.48 = bf16[2,8,176,128]{3,2,1,0:T(8,128)(2,1)S(1)} all-to-all(bf16[2,8,176,128]{3,2,1,0:T(8,128)(2,1)S(1)} %copy.428), channel_id=1, replica_groups=mesh['y'=4,'z'=8,'x'=4,'c'=2] {'c'}, dimensions={0} | all-to-all | bytes 1441792 | tf_op jit(solution)/shard_map/all_to_all | solution.py:39
  349.2 22.3 %all_to_all.49 = bf16[4,8,176,128]{3,2,1,0:T(8,128)(2,1)S(1)} all-to-all(bf16[4,8,176,128]{3,2,1,0:T(8,128)(2,1)S(1)} %pad_maximum_fusion), channel_id=1, replica_groups=mesh['y'=4,'z'=8,'x'=4,'c'=2] {'y'}, dimensions={0} | all-to-all | bytes 2883584 | tf_op jit(solution)/shard_map/all_to_all | solution.py:39
  371.8 16.3 %all_to_all.50 = bf16[8,176,128]{2,1,0:T(8,128)(2,1)S(1)} all-to-all(bf16[8,176,128]{2,1,0:T(8,128)(2,1)S(1)} %reduce_sum.294), channel_id=1, replica_groups=mesh['y'=4,'z'=8,'x'=4,'c'=2] {'z'}, dimensions={0} | all-to-all | bytes 720896 | tf_op jit(solution)/shard_map/all_to_all | solution.py:39
  (268 shorter events, 87.7 us)
Async XLA Ops:
  7.2 132.2 %all-gather.11.cloned.1.call-start = ((), (), s32[]{:S(2)}) async-start(), calls=%async_computation.9 | async-start | bytes 17039360 | tf_op jit(solution)/shard_map/all_gather | solution.py:73
  15.4 10.1 %all-to-all-start.2 = ((f32[4,32,160]{2,1,0:T(8,128)}), f32[4,32,160]{2,1,0:T(8,128)S(1)}, u32[]{:S(2)}, u32[]{:S(2)}) async-start(f32[4,32,160]{2,1,0:T(8,128)} %stack.30), calls=%async_computation.2 | async-start | bytes 262144 | tf_op jit(solution)/shard_map/all_to_all | solution.py:103
  23.9 7.1 %copy-start.40 = (f32[1,8192]{1,0:T(1,128)S(1)}, f32[1,8192]{1,0:T(1,128)}, u32[]{:S(2)}) copy-start(f32[1,8192]{1,0:T(1,128)} %param.15) | copy-start | bytes 98308
  25.5 31.3 %all-to-all-start = ((bf16[4,2,32,2048]{3,2,1,0:T(8,128)(2,1)}), bf16[4,2,32,2048]{3,2,1,0:T(8,128)(2,1)S(1)}, u32[]{:S(2)}, u32[]{:S(2)}) async-start(bf16[4,2,32,2048]{3,2,1,0:T(8,128)(2,1)} %reshape.261), calls=%async_computation | async-start | bytes 2097152 | tf_op jit(solution)/shard_map/all_to_all | solution.py:39
  37.2 5.8 %copy-start.30 = (bf16[1,160,512]{2,1,0:T(8,128)(2,1)S(1)}, bf16[1,160,512]{2,1,0:T(8,128)(2,1)}, u32[]{:S(2)}) copy-start(bf16[1,160,512]{2,1,0:T(8,128)(2,1)} %param.14) | copy-start | bytes 491524
  56.8 125.5 %copy-start = (bf16[4,160,512]{2,1,0:T(8,128)(2,1)}, bf16[4,160,512]{2,1,0:T(8,128)(2,1)S(1)}, u32[]{:S(2)}) copy-start(bf16[4,160,512]{2,1,0:T(8,128)(2,1)S(1)} %all_gather.59) | copy-start | bytes 1966084
  58.6 69.7 %all-to-all-start.1 = ((bf16[4,160,2048]{2,1,0:T(8,128)(2,1)}), bf16[4,160,2048]{2,1,0:T(8,128)(2,1)}, u32[]{:S(2)}, u32[]{:S(2)}) async-start(bf16[4,160,2048]{2,1,0:T(8,128)(2,1)} %broadcast_in_dim.33), calls=%async_computation.1 | async-start | bytes 5242880 | tf_op jit(solution)/shard_map/all_to_all | solution.py:39
  125.6 34.3 %copy-start.35 = (f32[1,1,2048]{2,1,0:T(1,128)}, f32[1,1,2048]{2,1,0:T(1,128)S(1)}, u32[]{:S(2)}) copy-start(f32[1,1,2048]{2,1,0:T(1,128)S(1)} %get-tuple-element.35) | copy-start | bytes 24580
  125.6 56.7 %copy-start.36 = (f32[1,1,2048]{2,1,0:T(1,128)}, f32[1,1,2048]{2,1,0:T(1,128)S(1)}, u32[]{:S(2)}) copy-start(f32[1,1,2048]{2,1,0:T(1,128)S(1)} %get-tuple-element.37) | copy-start | bytes 24580
  128.3 13.3 %copy-start.5 = (bf16[4,1,32,2048]{3,2,1,0:T(8,128)(2,1)}, bf16[4,1,32,2048]{3,2,1,0:T(8,128)(2,1)S(1)}, u32[]{:S(2)}) copy-start(bf16[4,1,32,2048]{3,2,1,0:T(8,128)(2,1)S(1)} %get-tuple-element.10) | copy-start | bytes 1572868
  189.8 21.1 %copy-start.38 = (f32[1,1,2048]{2,1,0:T(1,128)S(1)}, f32[1,1,2048]{2,1,0:T(1,128)}, u32[]{:S(2)}) copy-start(f32[1,1,2048]{2,1,0:T(1,128)} %get-tuple-element.34) | copy-start | bytes 24580
  242.1 4.4 %copy-start.15 = (bf16[128,2048]{1,0:T(8,128)(2,1)S(1)}, bf16[128,2048]{1,0:T(8,128)(2,1)}, u32[]{:S(2)}) copy-start(bf16[128,2048]{1,0:T(8,128)(2,1)} %get-tuple-element.3) | copy-start | bytes 1572868
  249.3 15.1 %copy-start.8 = (bf16[128,2048]{1,0:T(8,128)(2,1)}, bf16[128,2048]{1,0:T(8,128)(2,1)S(1)}, u32[]{:S(2)}) copy-start(bf16[128,2048]{1,0:T(8,128)(2,1)S(1)} %fusion.15) | copy-start | bytes 1572868
  249.3 16.2 %copy-start.1 = (bf16[4,160,512]{2,1,0:T(8,128)(2,1)S(1)}, bf16[4,160,512]{2,1,0:T(8,128)(2,1)}, u32[]{:S(2)}) copy-start(bf16[4,160,512]{2,1,0:T(8,128)(2,1)} %copy-done) | copy-start | bytes 1966084
  249.3 18.8 %copy-start.44 = (f32[128]{0:T(128)S(1)}, f32[128]{0:T(128)}, u32[]{:S(2)}) copy-start(f32[128]{0:T(128)} %copy-done.43) | copy-start | bytes 1540
  265.5 5.1 %copy-start.13 = (bf16[128,2048]{1,0:T(8,128)(2,1)S(1)}, bf16[128,2048]{1,0:T(8,128)(2,1)}, u32[]{:S(2)}) copy-start(bf16[128,2048]{1,0:T(8,128)(2,1)} %get-tuple-element.5) | copy-start | bytes 1572868
  273.3 15.1 %copy-start.7 = (bf16[128,2048]{1,0:T(8,128)(2,1)}, bf16[128,2048]{1,0:T(8,128)(2,1)S(1)}, u32[]{:S(2)}) copy-start(bf16[128,2048]{1,0:T(8,128)(2,1)S(1)} %fusion.16) | copy-start | bytes 1572868
  273.3 15.1 %copy-start.3 = (f32[128,802]{1,0:T(8,128)S(1)}, f32[128,802]{1,0:T(8,128)}, u32[]{:S(2)}) copy-start(f32[128,802]{1,0:T(8,128)} %copy-done.2) | copy-start | bytes 1231876
  273.3 15.8 %copy-start.20 = (f32[128,160]{0,1:T(8,128)S(1)}, f32[128,160]{0,1:T(8,128)}, u32[]{:S(2)}) copy-start(f32[128,160]{0,1:T(8,128)} %copy-done.19) | copy-start | bytes 245764
  273.4 18.0 %copy-start.42 = (f32[128]{0:T(128)S(1)}, f32[128]{0:T(128)}, u32[]{:S(2)}) copy-start(f32[128]{0:T(128)} %copy-done.41) | copy-start | bytes 1540
  289.2 4.5 %copy-start.29 = (f32[128,160]{0,1:T(8,128)S(1)}, f32[128,160]{0,1:T(8,128)}, u32[]{:S(2)}) copy-start(f32[128,160]{0,1:T(8,128)} %copy.476) | copy-start | bytes 245764
  289.2 4.5 %copy-start.31 = (bf16[128,128]{0,1:T(8,128)(2,1)S(1)}, bf16[128,128]{0,1:T(8,128)(2,1)}, u32[]{:S(2)}) copy-start(bf16[128,128]{0,1:T(8,128)(2,1)} %copy.442) | copy-start | bytes 98308
  289.2 4.5 %copy-start.32 = (bf16[128,128]{0,1:T(8,128)(2,1)S(1)}, bf16[128,128]{0,1:T(8,128)(2,1)}, u32[]{:S(2)}) copy-start(bf16[128,128]{0,1:T(8,128)(2,1)} %copy.443) | copy-start | bytes 98308
  289.2 4.5 %copy-start.33 = (bf16[128,128]{0,1:T(8,128)(2,1)S(1)}, bf16[128,128]{0,1:T(8,128)(2,1)}, u32[]{:S(2)}) copy-start(bf16[128,128]{0,1:T(8,128)(2,1)} %copy.444) | copy-start | bytes 98308
  289.2 4.5 %copy-start.34 = (bf16[128,128]{0,1:T(8,128)(2,1)S(1)}, bf16[128,128]{0,1:T(8,128)(2,1)}, u32[]{:S(2)}) copy-start(bf16[128,128]{0,1:T(8,128)(2,1)} %copy.445) | copy-start | bytes 98308
  289.2 4.5 %copy-start.46 = (f32[128]{0:T(128)S(1)}, f32[128]{0:T(128)}, u32[]{:S(2)}) copy-start(f32[128]{0:T(128)} %copy-done.45) | copy-start | bytes 1540
  327.2 16.1 %copy-start.10 = (bf16[2048,128]{1,0:T(8,128)(2,1)S(1)}, bf16[2048,128]{1,0:T(8,128)(2,1)}, u32[]{:S(2)}) copy-start(bf16[2048,128]{1,0:T(8,128)(2,1)} %copy.458) | copy-start | bytes 1572868
  327.2 16.1 %copy-start.48 = (f32[128]{0:T(128)S(1)}, f32[128]{0:T(128)}, u32[]{:S(2)}) copy-start(f32[128]{0:T(128)} %copy-done.47) | copy-start | bytes 1540
  329.9 14.0 %copy-start.24 = (bf16[128,160]{0,1:T(8,128)(2,1)S(1)}, bf16[128,160]{0,1:T(8,128)(2,1)}, u32[]{:S(2)}) copy-start(bf16[128,160]{0,1:T(8,128)(2,1)} %copy-done.23) | copy-start | bytes 122884
  344.2 4.8 %copy-start.16 = (bf16[8,176,128]{2,1,0:T(8,128)(2,1)S(1)}, bf16[8,176,128]{2,1,0:T(8,128)(2,1)}, u32[]{:S(2)}) copy-start(bf16[8,176,128]{2,1,0:T(8,128)(2,1)} %copy.487) | copy-start | bytes 1081348
  344.2 4.8 %copy-start.17 = (bf16[8,176,128]{2,1,0:T(8,128)(2,1)S(1)}, bf16[8,176,128]{2,1,0:T(8,128)(2,1)}, u32[]{:S(2)}) copy-start(bf16[8,176,128]{2,1,0:T(8,128)(2,1)} %copy.488) | copy-start | bytes 1081348
  344.2 4.8 %copy-start.18 = (bf16[8,176,128]{2,1,0:T(8,128)(2,1)S(1)}, bf16[8,176,128]{2,1,0:T(8,128)(2,1)}, u32[]{:S(2)}) copy-start(bf16[8,176,128]{2,1,0:T(8,128)(2,1)} %copy.489) | copy-start | bytes 1081348
  (27 other events, 78.1 us)
Sparse Core Ops, SparseCore 0:
  10.7 128.5 all-gather.10
